TPU v7x, 512 devices: a whole 4x8x8 slice. The times are simulated.
512 devices in a mesh: image: 16 (over z, x_hi), space: 32 (over y, x_lo, core).
Axes of the slice: x: 4 (x_hi: 2, x_lo: 2; x = x_hi * 2 + x_lo), y: 8, z: 8, core: 2. Of those that a mesh axis runs over, the one named last changes fastest.
Arguments:
- field: float32 [16, 128, 256, 512], P('image', 'space'), may hold values from -2.5 to 2.5
- mobility: float32 [128, 256, 512], P('space'), may hold values from 0.2 to 1
- fractions: float32 [16], P('image'), may hold values from 0.3 to 0.5
- sides: int32 [16], P('image'), may hold values from 0 to 1, as said below
Outputs:
- blended: float32 [16, 128, 256, 512], P('image', 'space')
Inputs may be any that keep to these rules, and one draw needn't show every extreme that they name: `sides`: the first image always names the next one (1), the last image the previous one (0); the others name either.
All inputs are finite; a program needn't handle non-finite values.
Results may differ from a plain program's by a relative error of at most 0.00002.
Values sent between devices are 32-bit elements; how exact they have to be, the bound alone decides.
A program may use at most 128 MiB of HBM per device.

v0:
```python
import jax
import jax.numpy as jnp
from jax import lax
from jax.sharding import PartitionSpec as P

STEPS = 4


DT = 0.1
EPS2 = 1.5


def with_halo(cells, sides, width):
    for axis, dim in sides:
        count = lax.axis_size(axis)
        ends = count - 1
        head = lax.slice_in_dim(cells, 0, width, axis=dim)
        tail = lax.slice_in_dim(cells, cells.shape[dim] - width, cells.shape[dim], axis=dim)
        cells = jnp.concatenate(
            [
                lax.ppermute(tail, axis, [(i, (i + 1) % count) for i in range(ends)]),
                cells,
                lax.ppermute(head, axis, [((i + 1) % count, i) for i in range(ends)]),
            ],
            axis=dim,
        )
    return cells


def passed_along(x, axis, by):
    devices = lax.axis_size(axis)
    pairs = [(i, i + by) for i in range(devices) if 0 <= i + by < devices]
    return lax.ppermute(x, axis, pairs)


def advance(phi, xpad, mob):
    padded = jnp.pad(xpad, ((0, 0), (1, 1), (1, 1)))
    beside = padded[2:, 1:-1, 1:-1] + padded[:-2, 1:-1, 1:-1]
    beside = beside + padded[1:-1, 2:, 1:-1] + padded[1:-1, :-2, 1:-1]
    beside = beside + padded[1:-1, 1:-1, 2:] + padded[1:-1, 1:-1, :-2]
    return phi + DT * mob * (EPS2 * (beside - 6.0 * phi) + phi - phi * phi * phi)


def local(field, mobility, fractions, sides):
    phi = field[0]
    for step in range(STEPS):
        xpad = with_halo(phi, (("space", 0),), 1)
        phi = advance(phi, xpad, mobility)
    upper = passed_along(phi, "image", -1)
    lower = passed_along(phi, "image", 1)
    neighbour = jnp.where(sides[0] == 1, upper, lower)
    blended = phi + fractions[0] * (neighbour - phi)
    return blended[None]


def solution(mesh):
    return jax.shard_map(
        local,
        mesh=mesh,
        in_specs=(P("image", "space", None, None), P("space", None, None), P("image"), P("image")),
        out_specs=P("image", "space", None, None),
        check_vma=False,
    )
```

profile of v0, /device:TPU:237, one launch (start us, length us, event | category | flops | bytes accessed | tf_op | source)
XLA Modules:
  0.0 181.4 jit_solution(14407894712745275566)
XLA Ops:
  0.0 0.0 copy-start.1
  0.0 1.4 slice_bitcast_fusion
  1.4 2.6 %collective-permute-start = (f32[1,256,512]{2,1,0:T(8,128)S(1)}, f32[1,256,512]{2,1,0:T(8,128)S(1)}, u32[]{:S(2)}, u32[]{:S(2)}) collective-permute-start(f32[1,256,512]{2,1,0:T(8,128)S(1)} %get-tuple-element.12), channel_id=1, source_target_pairs={{1,0},{2,1},{3,2},{4,3},{5,4},{6,5},{7,6},{8,7},{9,8},{10,9},{11,1... | collective-permute-start | bytes 1572872 | tf_op jit(solution)/shard_map/ppermute | solution.py:23
  4.0 3.0 %collective-permute-start.1 = (f32[1,256,512]{2,1,0:T(8,128)S(1)}, f32[1,256,512]{2,1,0:T(8,128)S(1)}, u32[]{:S(2)}, u32[]{:S(2)}) collective-permute-start(f32[1,256,512]{2,1,0:T(8,128)S(1)} %get-tuple-element.11), channel_id=1, source_target_pairs={{0,1},{1,2},{2,3},{3,4},{4,5},{5,6},{6,7},{7,8},{8,9},{9,10},{10,1... | collective-permute-start | bytes 1572872 | tf_op jit(solution)/shard_map/ppermute | solution.py:21
  7.0 10.5 %collective-permute-done = f32[1,256,512]{2,1,0:T(8,128)S(1)} collective-permute-done((f32[1,256,512]{2,1,0:T(8,128)S(1)}, f32[1,256,512]{2,1,0:T(8,128)S(1)}, u32[]{:S(2)}, u32[]{:S(2)}) %collective-permute-start) | collective-permute-done | bytes 524320 | tf_op jit(solution)/shard_map/ppermute | solution.py:23
  17.5 0.0 collective-permute-done.1
  17.5 0.0 copy-done.1
  17.5 0.0 copy-start
  17.6 2.3 %select_maximum_fusion.6 = f32[6,258,514]{2,1,0:T(8,128)S(1)} fusion(f32[1,256,512]{2,1,0:T(8,128)S(1)} %collective-permute-done, f32[4,256,512]{2,1,0:T(8,128)S(1)} %bitcast.10, f32[1,256,512]{2,1,0:T(8,128)S(1)} %collective-permute-done.1), kind=kLoop, calls=%fused_computation.10 | loop fusion | flops 11935080 | bytes 6328416 | tf_op jit(solution)/shard_map/concatenate | solution.py:19
  19.8 0.0 copy-done
  19.9 2.3 %fusion.5 = f32[4,256,512]{2,1,0:T(8,128)S(1)} fusion(f32[4,256,512]{2,1,0:T(8,128)S(1)} %bitcast.11, f32[6,258,514]{2,1,0:T(8,128)S(1)} %select_maximum_fusion.6, f32[1,256,512]{2,1,0:T(8,128)S(1)} %collective-permute-done.1, f32[1,256,512]{2,1,0:T(8,128)S(1)} %collective-permute-done, f32[4,256,512]{2,1,0:T(8,128)S(1)} %copy-done), kind=kLoop, calls=%fused_computation.21 | loop fusion | flops 8912896 | bytes 15728640 | tf_op jit(solution)/shard_map/add | solution.py:41
  22.1 0.1 fusion.33
  22.2 1.9 %collective-permute-start.2 = (f32[1,256,512]{2,1,0:T(8,128)S(1)}, f32[1,256,512]{2,1,0:T(8,128)S(1)}, u32[]{:S(2)}, u32[]{:S(2)}) collective-permute-start(f32[1,256,512]{2,1,0:T(8,128)S(1)} %get-tuple-element.10), channel_id=1, source_target_pairs={{1,0},{2,1},{3,2},{4,3},{5,4},{6,5},{7,6},{8,7},{9,8},{10,9},{11,1... | collective-permute-start | bytes 1572872 | tf_op jit(solution)/shard_map/ppermute | solution.py:23
  24.1 4.3 %collective-permute-start.3 = (f32[1,256,512]{2,1,0:T(8,128)S(1)}, f32[1,256,512]{2,1,0:T(8,128)S(1)}, u32[]{:S(2)}, u32[]{:S(2)}) collective-permute-start(f32[1,256,512]{2,1,0:T(8,128)S(1)} %get-tuple-element.9), channel_id=1, source_target_pairs={{0,1},{1,2},{2,3},{3,4},{4,5},{5,6},{6,7},{7,8},{8,9},{9,10},{10,1... | collective-permute-start | bytes 1572872 | tf_op jit(solution)/shard_map/ppermute | solution.py:21
  28.4 10.5 %collective-permute-done.2 = f32[1,256,512]{2,1,0:T(8,128)S(1)} collective-permute-done((f32[1,256,512]{2,1,0:T(8,128)S(1)}, f32[1,256,512]{2,1,0:T(8,128)S(1)}, u32[]{:S(2)}, u32[]{:S(2)}) %collective-permute-start.2) | collective-permute-done | bytes 524320 | tf_op jit(solution)/shard_map/ppermute | solution.py:23
  39.0 0.0 collective-permute-done.3
  39.0 2.3 %select_maximum_fusion.4 = f32[6,258,514]{2,1,0:T(8,128)S(1)} fusion(f32[1,256,512]{2,1,0:T(8,128)S(1)} %collective-permute-done.2, f32[4,256,512]{2,1,0:T(8,128)S(1)} %fusion.5, f32[1,256,512]{2,1,0:T(8,128)S(1)} %collective-permute-done.3), kind=kLoop, calls=%fused_computation.8 | loop fusion | flops 11935080 | bytes 6328416 | tf_op jit(solution)/shard_map/concatenate | solution.py:19
  41.2 2.3 %fusion.8 = f32[4,256,512]{2,1,0:T(8,128)S(1)} fusion(f32[4,256,512]{2,1,0:T(8,128)S(1)} %fusion.5, f32[6,258,514]{2,1,0:T(8,128)S(1)} %select_maximum_fusion.4, f32[1,256,512]{2,1,0:T(8,128)S(1)} %collective-permute-done.3, f32[1,256,512]{2,1,0:T(8,128)S(1)} %collective-permute-done.2, f32[4,256,512]{2,1,0:T(8,128)S(1)} %copy-done), kind=kLoop, calls=%fused_computation.24 | loop fusion | flops 8912896 | bytes 15728640 | tf_op jit(solution)/shard_map/add | solution.py:41
  43.5 0.1 fusion.32
  43.6 1.9 %collective-permute-start.4 = (f32[1,256,512]{2,1,0:T(8,128)S(1)}, f32[1,256,512]{2,1,0:T(8,128)S(1)}, u32[]{:S(2)}, u32[]{:S(2)}) collective-permute-start(f32[1,256,512]{2,1,0:T(8,128)S(1)} %get-tuple-element.8), channel_id=1, source_target_pairs={{1,0},{2,1},{3,2},{4,3},{5,4},{6,5},{7,6},{8,7},{9,8},{10,9},{11,1... | collective-permute-start | bytes 1572872 | tf_op jit(solution)/shard_map/ppermute | solution.py:23
  45.5 3.6 %collective-permute-start.5 = (f32[1,256,512]{2,1,0:T(8,128)S(1)}, f32[1,256,512]{2,1,0:T(8,128)S(1)}, u32[]{:S(2)}, u32[]{:S(2)}) collective-permute-start(f32[1,256,512]{2,1,0:T(8,128)S(1)} %get-tuple-element.7), channel_id=1, source_target_pairs={{0,1},{1,2},{2,3},{3,4},{4,5},{5,6},{6,7},{7,8},{8,9},{9,10},{10,1... | collective-permute-start | bytes 1572872 | tf_op jit(solution)/shard_map/ppermute | solution.py:21
  49.2 10.5 %collective-permute-done.4 = f32[1,256,512]{2,1,0:T(8,128)S(1)} collective-permute-done((f32[1,256,512]{2,1,0:T(8,128)S(1)}, f32[1,256,512]{2,1,0:T(8,128)S(1)}, u32[]{:S(2)}, u32[]{:S(2)}) %collective-permute-start.4) | collective-permute-done | bytes 524320 | tf_op jit(solution)/shard_map/ppermute | solution.py:23
  59.7 0.0 collective-permute-done.5
  59.7 2.3 %select_maximum_fusion.2 = f32[6,258,514]{2,1,0:T(8,128)S(1)} fusion(f32[1,256,512]{2,1,0:T(8,128)S(1)} %collective-permute-done.4, f32[4,256,512]{2,1,0:T(8,128)S(1)} %fusion.8, f32[1,256,512]{2,1,0:T(8,128)S(1)} %collective-permute-done.5), kind=kLoop, calls=%fused_computation.6 | loop fusion | flops 11935080 | bytes 6328416 | tf_op jit(solution)/shard_map/concatenate | solution.py:19
  62.0 2.3 %fusion.11 = f32[4,256,512]{2,1,0:T(8,128)S(1)} fusion(f32[4,256,512]{2,1,0:T(8,128)S(1)} %fusion.8, f32[6,258,514]{2,1,0:T(8,128)S(1)} %select_maximum_fusion.2, f32[1,256,512]{2,1,0:T(8,128)S(1)} %collective-permute-done.5, f32[1,256,512]{2,1,0:T(8,128)S(1)} %collective-permute-done.4, f32[4,256,512]{2,1,0:T(8,128)S(1)} %copy-done), kind=kLoop, calls=%fused_computation.27 | loop fusion | flops 8912896 | bytes 15728640 | tf_op jit(solution)/shard_map/add | solution.py:41
  64.3 0.1 fusion.31
  64.4 1.9 %collective-permute-start.6 = (f32[1,256,512]{2,1,0:T(8,128)S(1)}, f32[1,256,512]{2,1,0:T(8,128)S(1)}, u32[]{:S(2)}, u32[]{:S(2)}) collective-permute-start(f32[1,256,512]{2,1,0:T(8,128)S(1)} %get-tuple-element.6), channel_id=1, source_target_pairs={{1,0},{2,1},{3,2},{4,3},{5,4},{6,5},{7,6},{8,7},{9,8},{10,9},{11,1... | collective-permute-start | bytes 1572872 | tf_op jit(solution)/shard_map/ppermute | solution.py:23
  66.3 3.6 %collective-permute-start.7 = (f32[1,256,512]{2,1,0:T(8,128)S(1)}, f32[1,256,512]{2,1,0:T(8,128)S(1)}, u32[]{:S(2)}, u32[]{:S(2)}) collective-permute-start(f32[1,256,512]{2,1,0:T(8,128)S(1)} %get-tuple-element.5), channel_id=1, source_target_pairs={{0,1},{1,2},{2,3},{3,4},{4,5},{5,6},{6,7},{7,8},{8,9},{9,10},{10,1... | collective-permute-start | bytes 1572872 | tf_op jit(solution)/shard_map/ppermute | solution.py:21
  69.9 10.5 %collective-permute-done.6 = f32[1,256,512]{2,1,0:T(8,128)S(1)} collective-permute-done((f32[1,256,512]{2,1,0:T(8,128)S(1)}, f32[1,256,512]{2,1,0:T(8,128)S(1)}, u32[]{:S(2)}, u32[]{:S(2)}) %collective-permute-start.6) | collective-permute-done | bytes 524320 | tf_op jit(solution)/shard_map/ppermute | solution.py:23
  80.5 0.0 collective-permute-done.7
  80.5 2.3 %select_maximum_fusion = f32[6,258,514]{2,1,0:T(8,128)S(1)} fusion(f32[1,256,512]{2,1,0:T(8,128)S(1)} %collective-permute-done.6, f32[4,256,512]{2,1,0:T(8,128)S(1)} %fusion.11, f32[1,256,512]{2,1,0:T(8,128)S(1)} %collective-permute-done.7), kind=kLoop, calls=%fused_computation.4 | loop fusion | flops 11935080 | bytes 6328416 | tf_op jit(solution)/shard_map/concatenate | solution.py:19
  82.7 2.3 %fusion.14 = f32[4,256,512]{2,1,0:T(8,128)S(1)} fusion(f32[4,256,512]{2,1,0:T(8,128)S(1)} %fusion.11, f32[6,258,514]{2,1,0:T(8,128)S(1)} %select_maximum_fusion, f32[1,256,512]{2,1,0:T(8,128)S(1)} %collective-permute-done.7, f32[1,256,512]{2,1,0:T(8,128)S(1)} %collective-permute-done.6, f32[4,256,512]{2,1,0:T(8,128)S(1)} %copy-done), kind=kLoop, calls=%fused_computation.30 | loop fusion | flops 8912896 | bytes 15728640 | tf_op jit(solution)/shard_map/add | solution.py:41
  85.0 2.4 %collective-permute-start.8 = (f32[4,256,512]{2,1,0:T(8,128)S(1)}, f32[4,256,512]{2,1,0:T(8,128)S(1)}, u32[]{:S(2)}, u32[]{:S(2)}) collective-permute-start(f32[4,256,512]{2,1,0:T(8,128)S(1)} %fusion.14), channel_id=1, source_target_pairs={{32,0},{64,32},{96,64},{128,96},{160,128},{192,160},{224,192},{256... | collective-permute-start | bytes 6291464 | tf_op jit(solution)/shard_map/ppermute | solution.py:33
  87.5 6.5 %collective-permute-start.9 = (f32[4,256,512]{2,1,0:T(8,128)S(1)}, f32[4,256,512]{2,1,0:T(8,128)S(1)}, u32[]{:S(2)}, u32[]{:S(2)}) collective-permute-start(f32[4,256,512]{2,1,0:T(8,128)S(1)} %fusion.14), channel_id=1, source_target_pairs={{0,32},{32,64},{64,96},{96,128},{128,160},{160,192},{192,224},{224... | collective-permute-start | bytes 6291464 | tf_op jit(solution)/shard_map/ppermute | solution.py:33
  95.2 78.9 %collective-permute-done.8 = f32[4,256,512]{2,1,0:T(8,128)S(1)} collective-permute-done((f32[4,256,512]{2,1,0:T(8,128)S(1)}, f32[4,256,512]{2,1,0:T(8,128)S(1)}, u32[]{:S(2)}, u32[]{:S(2)}) %collective-permute-start.8) | collective-permute-done | bytes 2097184 | tf_op jit(solution)/shard_map/ppermute | solution.py:33
  174.1 5.2 %collective-permute-done.9 = f32[4,256,512]{2,1,0:T(8,128)S(1)} collective-permute-done((f32[4,256,512]{2,1,0:T(8,128)S(1)}, f32[4,256,512]{2,1,0:T(8,128)S(1)}, u32[]{:S(2)}, u32[]{:S(2)}) %collective-permute-start.9) | collective-permute-done | bytes 2097184 | tf_op jit(solution)/shard_map/ppermute | solution.py:33
  179.3 2.1 %add_bitcast_fusion = f32[1,4,256,512]{3,2,1,0:T(8,128)} fusion(f32[4,256,512]{2,1,0:T(8,128)S(1)} %fusion.14, f32[4,256,512]{2,1,0:T(8,128)S(1)} %collective-permute-done.8, f32[4,256,512]{2,1,0:T(8,128)S(1)} %collective-permute-done.9, f32[]{:T(128)} %bitcast.9, pred[]{:T(512)} %bitcast.4), kind=kLoop, calls=%fused_computation.71 | loop fusion | flops 2097152 | bytes 8388613 | tf_op jit(solution)/shard_map/broadcast_in_dim | solution.py:53
Async XLA Ops:
  0.0 17.5 %copy-start.1 = (f32[1,4,256,512]{3,2,1,0:T(8,128)S(1)}, f32[1,4,256,512]{3,2,1,0:T(8,128)}, u32[]{:S(2)}) copy-start(f32[1,4,256,512]{3,2,1,0:T(8,128)} %param.4) | copy-start | bytes 6291460
  1.4 16.1 %collective-permute-start = (f32[1,256,512]{2,1,0:T(8,128)S(1)}, f32[1,256,512]{2,1,0:T(8,128)S(1)}, u32[]{:S(2)}, u32[]{:S(2)}) collective-permute-start(f32[1,256,512]{2,1,0:T(8,128)S(1)} %get-tuple-element.12), channel_id=1, source_target_pairs={{1,0},{2,1},{3,2},{4,3},{5,4},{6,5},{7,6},{8,7},{9,8},{10,9},{11,1... | collective-permute-start | bytes 1572872 | tf_op jit(solution)/shard_map/ppermute | solution.py:23
  4.0 13.5 %collective-permute-start.1 = (f32[1,256,512]{2,1,0:T(8,128)S(1)}, f32[1,256,512]{2,1,0:T(8,128)S(1)}, u32[]{:S(2)}, u32[]{:S(2)}) collective-permute-start(f32[1,256,512]{2,1,0:T(8,128)S(1)} %get-tuple-element.11), channel_id=1, source_target_pairs={{0,1},{1,2},{2,3},{3,4},{4,5},{5,6},{6,7},{7,8},{8,9},{9,10},{10,1... | collective-permute-start | bytes 1572872 | tf_op jit(solution)/shard_map/ppermute | solution.py:21
  17.5 2.3 %copy-start = (f32[4,256,512]{2,1,0:T(8,128)S(1)}, f32[4,256,512]{2,1,0:T(8,128)}, u32[]{:S(2)}) copy-start(f32[4,256,512]{2,1,0:T(8,128)} %param.5) | copy-start | bytes 6291460
  22.2 16.7 %collective-permute-start.2 = (f32[1,256,512]{2,1,0:T(8,128)S(1)}, f32[1,256,512]{2,1,0:T(8,128)S(1)}, u32[]{:S(2)}, u32[]{:S(2)}) collective-permute-start(f32[1,256,512]{2,1,0:T(8,128)S(1)} %get-tuple-element.10), channel_id=1, source_target_pairs={{1,0},{2,1},{3,2},{4,3},{5,4},{6,5},{7,6},{8,7},{9,8},{10,9},{11,1... | collective-permute-start | bytes 1572872 | tf_op jit(solution)/shard_map/ppermute | solution.py:23
  24.1 14.8 %collective-permute-start.3 = (f32[1,256,512]{2,1,0:T(8,128)S(1)}, f32[1,256,512]{2,1,0:T(8,128)S(1)}, u32[]{:S(2)}, u32[]{:S(2)}) collective-permute-start(f32[1,256,512]{2,1,0:T(8,128)S(1)} %get-tuple-element.9), channel_id=1, source_target_pairs={{0,1},{1,2},{2,3},{3,4},{4,5},{5,6},{6,7},{7,8},{8,9},{9,10},{10,1... | collective-permute-start | bytes 1572872 | tf_op jit(solution)/shard_map/ppermute | solution.py:21
  43.6 16.1 %collective-permute-start.4 = (f32[1,256,512]{2,1,0:T(8,128)S(1)}, f32[1,256,512]{2,1,0:T(8,128)S(1)}, u32[]{:S(2)}, u32[]{:S(2)}) collective-permute-start(f32[1,256,512]{2,1,0:T(8,128)S(1)} %get-tuple-element.8), channel_id=1, source_target_pairs={{1,0},{2,1},{3,2},{4,3},{5,4},{6,5},{7,6},{8,7},{9,8},{10,9},{11,1... | collective-permute-start | bytes 1572872 | tf_op jit(solution)/shard_map/ppermute | solution.py:23
  45.5 14.2 %collective-permute-start.5 = (f32[1,256,512]{2,1,0:T(8,128)S(1)}, f32[1,256,512]{2,1,0:T(8,128)S(1)}, u32[]{:S(2)}, u32[]{:S(2)}) collective-permute-start(f32[1,256,512]{2,1,0:T(8,128)S(1)} %get-tuple-element.7), channel_id=1, source_target_pairs={{0,1},{1,2},{2,3},{3,4},{4,5},{5,6},{6,7},{7,8},{8,9},{9,10},{10,1... | collective-permute-start | bytes 1572872 | tf_op jit(solution)/shard_map/ppermute | solution.py:21
  64.4 16.1 %collective-permute-start.6 = (f32[1,256,512]{2,1,0:T(8,128)S(1)}, f32[1,256,512]{2,1,0:T(8,128)S(1)}, u32[]{:S(2)}, u32[]{:S(2)}) collective-permute-start(f32[1,256,512]{2,1,0:T(8,128)S(1)} %get-tuple-element.6), channel_id=1, source_target_pairs={{1,0},{2,1},{3,2},{4,3},{5,4},{6,5},{7,6},{8,7},{9,8},{10,9},{11,1... | collective-permute-start | bytes 1572872 | tf_op jit(solution)/shard_map/ppermute | solution.py:23
  66.3 14.2 %collective-permute-start.7 = (f32[1,256,512]{2,1,0:T(8,128)S(1)}, f32[1,256,512]{2,1,0:T(8,128)S(1)}, u32[]{:S(2)}, u32[]{:S(2)}) collective-permute-start(f32[1,256,512]{2,1,0:T(8,128)S(1)} %get-tuple-element.5), channel_id=1, source_target_pairs={{0,1},{1,2},{2,3},{3,4},{4,5},{5,6},{6,7},{7,8},{8,9},{9,10},{10,1... | collective-permute-start | bytes 1572872 | tf_op jit(solution)/shard_map/ppermute | solution.py:21
  85.0 89.1 %collective-permute-start.8 = (f32[4,256,512]{2,1,0:T(8,128)S(1)}, f32[4,256,512]{2,1,0:T(8,128)S(1)}, u32[]{:S(2)}, u32[]{:S(2)}) collective-permute-start(f32[4,256,512]{2,1,0:T(8,128)S(1)} %fusion.14), channel_id=1, source_target_pairs={{32,0},{64,32},{96,64},{128,96},{160,128},{192,160},{224,192},{256... | collective-permute-start | bytes 6291464 | tf_op jit(solution)/shard_map/ppermute | solution.py:33
  87.5 91.8 %collective-permute-start.9 = (f32[4,256,512]{2,1,0:T(8,128)S(1)}, f32[4,256,512]{2,1,0:T(8,128)S(1)}, u32[]{:S(2)}, u32[]{:S(2)}) collective-permute-start(f32[4,256,512]{2,1,0:T(8,128)S(1)} %fusion.14), channel_id=1, source_target_pairs={{0,32},{32,64},{64,96},{96,128},{128,160},{160,192},{192,224},{224... | collective-permute-start | bytes 6291464 | tf_op jit(solution)/shard_map/ppermute | solution.py:33
where the time goes:
time: 182 us; the launch traced here: 181 us
  waiting for transfers between devices  126 us (69%)
  starting transfers between devices  31.8 us (17%)
  other arithmetic  20.3 us (11%)
    ppermute x2, waiting for transfers between devices, passed_along(): return lax.ppermute(x, axis, pairs)  84 us
    ppermute x4, waiting for transfers between devices, with_halo(): lax.ppermute(head, axis, [((i + 1) % count, i) for i in range(ends)])  42.2 us
    ppermute x4, starting transfers between devices, with_halo(): lax.ppermute(tail, axis, [(i, (i + 1) % count) for i in range(ends)])  14.5 us
    add x4, other arithmetic, advance(): phi + DT * mob * (EPS2 * (beside - 6.0 * phi) + phi - phi * phi * phi)  9.1 us
    concatenate x4, other arithmetic, with_halo(): jnp.concatenate([lax.ppermute(tail, axis, [(i, (i + 1) % count) for i in...  9.07 us
    ppermute x2, starting transfers between devices, passed_along(): return lax.ppermute(x, axis, pairs)  8.9 us
    ppermute x4, starting transfers between devices, with_halo(): lax.ppermute(head, axis, [((i + 1) % count, i) for i in range(ends)])  8.35 us
  transfers between devices with their start and end apart: 10, of which 6 were waited for; matrix products, arithmetic and copies ran while one was open for 0% of the time, Pallas kernels for 0%

commit v1 on v0

v1 whole, which is shorter than its diff:
```python
import functools

import jax
import jax.numpy as jnp
from jax import lax
from jax.experimental import pallas as pl
from jax.experimental.pallas import tpu as pltpu
from jax.sharding import PartitionSpec as P

STEPS = 4
DT = 0.1
EPS2 = 1.5
PAD = 8


def kernel(
    cfg, field, mobility, frac, sides, out,
    phi, mob, xbuf, zbuf, obuf,
    load_sem, hs, hr, xs, xr, zs, zr, osem,
):
    images, spaces, planes, ny, nz, nc = cfg
    rows = ny // nc
    img = lax.axis_index("image")
    sp = lax.axis_index("space")
    hi = lax.rem(img, 2)
    partner = img + 1 - 2 * hi
    z_to = img + 2 - 4 * hi
    z_from = img - 2 + 4 * hi
    has_l = sp > 0
    has_r = sp < spaces - 1
    has_to = jnp.logical_and(z_to >= 0, z_to < images)
    has_from = jnp.logical_and(z_from >= 0, z_from < images)
    first, last = 1, planes

    def own(t, p, c):
        return phi.at[t, p, pl.ds(PAD + pl.multiple_of(c * rows, 8), rows)]

    def seg(ref, p, c):
        return ref.at[p, pl.ds(pl.multiple_of(c * rows, 8), rows)]

    def halo(t, side, c):
        return pltpu.make_async_remote_copy(
            src_ref=own(t, last if side == 0 else first, c),
            dst_ref=own(t, 0 if side == 0 else planes + 1, c),
            send_sem=hs.at[t, side, c],
            recv_sem=hr.at[t, side, c],
            device_id={"space": sp + 1 if side == 0 else sp - 1},
            device_id_type=pl.DeviceIdType.MESH,
        )

    def xcopy(p, c):
        return pltpu.make_async_remote_copy(
            src_ref=own(STEPS, p + 1, c),
            dst_ref=seg(xbuf, p, c),
            send_sem=xs.at[p, c],
            recv_sem=xr.at[p, c],
            device_id={"image": partner},
            device_id_type=pl.DeviceIdType.MESH,
        )

    def zcopy(p, c):
        return pltpu.make_async_remote_copy(
            src_ref=seg(xbuf, p, c),
            dst_ref=seg(zbuf, p, c),
            send_sem=zs.at[p, c],
            recv_sem=zr.at[p, c],
            device_id={"image": z_to},
            device_id_type=pl.DeviceIdType.MESH,
        )

    def ocopy(p, c):
        return pltpu.make_async_copy(seg(obuf, p, c), seg(out.at[0], p, c), osem.at[p, c])

    def send_halo(t, c):
        @pl.when(has_r)
        def _():
            halo(t, 0, c).start()

        @pl.when(has_l)
        def _():
            halo(t, 1, c).start()

    def wait_halo(t, c):
        @pl.when(has_l)
        def _():
            halo(t, 0, c).wait_recv()

        @pl.when(has_r)
        def _():
            halo(t, 1, c).wait_recv()

    lane = lax.broadcasted_iota(jnp.int32, (rows, nz), 1)

    def advance(t, p, c):
        r0 = PAD + pl.multiple_of(c * rows, 8)
        here = phi[t, p, pl.ds(r0, rows)]
        s = phi[t, p - 1, pl.ds(r0, rows)] + phi[t, p + 1, pl.ds(r0, rows)]
        wide = phi[t, p, pl.ds(r0 - 8, rows + 16)]
        s = s + wide[7 : 7 + rows] + wide[9 : 9 + rows]
        s = s + jnp.where(lane == 0, 0.0, pltpu.roll(here, 1, 1))
        s = s + jnp.where(lane == nz - 1, 0.0, pltpu.roll(here, nz - 1, 1))
        m = mob[p - 1, pl.ds(pl.multiple_of(c * rows, 8), rows)]
        phi[t + 1, p, pl.ds(r0, rows)] = here + m * (EPS2 * s - here * (8.0 + here * here))

    loads = [pltpu.make_async_copy(field.at[0, p], phi.at[0, p + 1, pl.ds(PAD, ny)], load_sem.at[p]) for p in range(planes)]
    loads.append(pltpu.make_async_copy(mobility, mob, load_sem.at[planes]))
    for copy in (loads[0], loads[planes - 1], *loads[1 : planes - 1], loads[planes]):
        copy.start()

    barrier = pltpu.get_barrier_semaphore()

    def greet(axis, where, known):
        @pl.when(known)
        def _():
            pl.semaphore_signal(barrier, 1, device_id={axis: where}, device_id_type=pl.DeviceIdType.MESH)

    greet("space", sp + 1, has_r)
    greet("space", sp - 1, has_l)
    pl.semaphore_signal(barrier, 1, device_id={"image": partner}, device_id_type=pl.DeviceIdType.MESH)
    greet("image", z_to, has_to)
    greet("image", z_from, has_from)

    def clear_rows(t, _):
        for p in range(1, planes + 1):
            phi[t, p, pl.ds(0, PAD)] = jnp.zeros((PAD, nz), jnp.float32)
            phi[t, p, pl.ds(PAD + ny, PAD)] = jnp.zeros((PAD, nz), jnp.float32)
        return 0

    lax.fori_loop(0, STEPS, clear_rows, 0)

    def clear_halo(plane):
        def body(i, _):
            phi[i // nc, plane, pl.ds(PAD + pl.multiple_of(lax.rem(i, nc) * rows, 8), rows)] = jnp.zeros((rows, nz), jnp.float32)
            return 0

        lax.fori_loop(0, STEPS * nc, body, 0)

    @pl.when(jnp.logical_not(has_l))
    def _():
        clear_halo(0)

    @pl.when(jnp.logical_not(has_r))
    def _():
        clear_halo(planes + 1)

    @pl.when(jnp.logical_not(has_from))
    def _():
        def body(i, _):
            zbuf[i // nc, pl.ds(pl.multiple_of(lax.rem(i, nc) * rows, 8), rows)] = jnp.zeros((rows, nz), jnp.float32)
            return 0

        lax.fori_loop(0, planes * nc, body, 0)

    loads[0].wait()
    loads[planes - 1].wait()
    one = lambda flag: jnp.where(flag, 1, 0)
    pl.semaphore_wait(barrier, 1 + one(has_l) + one(has_r) + one(has_to) + one(has_from))

    for c in range(nc):
        send_halo(0, c)
    for p in range(1, planes - 1):
        loads[p].wait()
    loads[planes].wait()

    def scale(i, _):
        at = (i // nc, pl.ds(pl.multiple_of(lax.rem(i, nc) * rows, 8), rows))
        mob[at] = DT * mob[at]
        return 0

    lax.fori_loop(0, planes * nc, scale, 0)

    def chunk(i, _):
        t, c = i // nc, lax.rem(i, nc)
        wait_halo(t, c)
        advance(t, first, c)
        advance(t, last, c)
        for p in range(first + 1, last):
            advance(t, p, c)
        send_halo(t + 1, c)
        return 0

    lax.fori_loop(0, (STEPS - 1) * nc, chunk, 0)

    end = STEPS - 1

    def inner(c, _):
        for p in range(first + 1, last):
            advance(end, p, c)
        for p in range(first + 1, last):
            xcopy(p - 1, c).start()
        return 0

    lax.fori_loop(0, nc, inner, 0)

    def outer(c, _):
        wait_halo(end, c)
        advance(end, first, c)
        advance(end, last, c)
        xcopy(first - 1, c).start()
        xcopy(last - 1, c).start()
        return 0

    lax.fori_loop(0, nc, outer, 0)

    f = frac[0]
    use_x = sides[0] != hi
    lag = 3
    units = planes * nc

    def unit(u):
        half = u // (2 * nc)
        v = lax.rem(u, 2 * nc)
        odd = lax.rem(v, 2)
        p = jnp.where(half == 0, 1 + odd, 3 * odd)
        return p, v // 2

    def relay(u, _):
        @pl.when(u < units)
        def _():
            p, c = unit(u)
            xcopy(p, c).wait_recv()

            @pl.when(has_to)
            def _():
                zcopy(p, c).start()

        @pl.when(u >= lag)
        def _():
            p, c = unit(u - lag)

            @pl.when(has_from)
            def _():
                zcopy(p, c).wait_recv()

            at = (p, pl.ds(pl.multiple_of(c * rows, 8), rows))
            mine = phi[STEPS, p + 1, pl.ds(PAD + pl.multiple_of(c * rows, 8), rows)]
            other = jnp.where(use_x, xbuf[at], zbuf[at])
            obuf[at] = mine + f * (other - mine)
            ocopy(p, c).start()

        return 0

    lax.fori_loop(0, units + lag, relay, 0)

    def drain_halo(i, _):
        t, c = i // nc, lax.rem(i, nc)

        @pl.when(has_r)
        def _():
            halo(t, 0, c).wait_send()

        @pl.when(has_l)
        def _():
            halo(t, 1, c).wait_send()

        return 0

    lax.fori_loop(0, STEPS * nc, drain_halo, 0)

    def drain(i, _):
        p, c = i // nc, lax.rem(i, nc)
        xcopy(p, c).wait_send()

        @pl.when(has_to)
        def _():
            zcopy(p, c).wait_send()

        ocopy(p, c).wait()
        return 0

    lax.fori_loop(0, units, drain, 0)


def local(images, spaces, field, mobility, fractions, sides):
    _, planes, ny, nz = field.shape
    nc = 4
    cfg = (images, spaces, planes, ny, nz, nc)
    dma = pltpu.SemaphoreType.DMA
    return pl.pallas_call(
        functools.partial(kernel, cfg),
        out_shape=jax.ShapeDtypeStruct(field.shape, jnp.float32),
        in_specs=[
            pl.BlockSpec(memory_space=pl.ANY),
            pl.BlockSpec(memory_space=pl.ANY),
            pl.BlockSpec(memory_space=pltpu.SMEM),
            pl.BlockSpec(memory_space=pltpu.SMEM),
        ],
        out_specs=pl.BlockSpec(memory_space=pl.ANY),
        scratch_shapes=[
            pltpu.VMEM((STEPS + 1, planes + 2, ny + 2 * PAD, nz), jnp.float32),
            pltpu.VMEM((planes, ny, nz), jnp.float32),
            pltpu.VMEM((planes, ny, nz), jnp.float32),
            pltpu.VMEM((planes, ny, nz), jnp.float32),
            pltpu.VMEM((planes, ny, nz), jnp.float32),
            dma((planes + 1,)),
            dma((STEPS, 2, nc)),
            dma((STEPS, 2, nc)),
            dma((planes, nc)),
            dma((planes, nc)),
            dma((planes, nc)),
            dma((planes, nc)),
            dma((planes, nc)),
        ],
        compiler_params=pltpu.CompilerParams(
            collective_id=0, has_side_effects=True, vmem_limit_bytes=48 * 1024 * 1024
        ),
    )(field, mobility, fractions, sides)


def solution(mesh):
    return jax.shard_map(
        functools.partial(local, mesh.shape["image"], mesh.shape["space"]),
        mesh=mesh,
        in_specs=(P("image", "space", None, None), P("space", None, None), P("image"), P("image")),
        out_specs=P("image", "space", None, None),
        check_vma=False,
    )
```

time: 182 us -> 113 us (0.62)
  the two profiles are of different devices: /device:TPU:237 before, /device:TPU:181 now
where the time goes in v1:
time: 113 us; the launch traced here: 112 us
  Pallas kernels  108 us (96%)
  local copies, waits for them, and re-layouts  2.91 us (3%)
  between operations  1.31 us (1%)
    pallas_call x1, Pallas kernels, local(): pl.pallas_call(functools.partial(kernel, cfg), out_shape=jax.ShapeDtypeSt...  108 us
    unnamed x3, local copies, waits for them, and re-layouts  2.91 us

profile of v1, /device:TPU:181, one launch (start us, length us, event | category | flops | bytes accessed | tf_op | source)
XLA Modules:
  0.0 112.4 jit_solution(8853762132518168136)
XLA Ops:
  1.3 0.0 copy-start
  1.3 1.6 %copy-done = f32[1,4,256,512]{3,2,1,0:T(8,128)S(1)} copy-done((f32[1,4,256,512]{3,2,1,0:T(8,128)S(1)}, f32[1,4,256,512]{3,2,1,0:T(8,128)}, u32[]{:S(2)}) %copy-start) | copy-done | bytes 2097176
  2.9 108.2 %shard_map.46 = f32[1,4,256,512]{3,2,1,0:T(8,128)S(1)} custom-call(f32[1,4,256,512]{3,2,1,0:T(8,128)S(1)} %copy-done, f32[4,256,512]{2,1,0:T(8,128)} %mobility.1, f32[1]{0:T(128)S(6)} %copy.6.frac, s32[1]{0:T(128)S(6)} %copy.7.sides), custom_call_target="tpu_custom_call" | custom-call | tf_op jit(solution)/shard_map/pallas_call | solution.py:279
  111.1 1.3 %copy.8 = f32[1,4,256,512]{3,2,1,0:T(8,128)} copy(f32[1,4,256,512]{3,2,1,0:T(8,128)S(1)} %shard_map.46) | data formatting | bytes 4194304
Async XLA Ops:
  1.3 1.6 %copy-start = (f32[1,4,256,512]{3,2,1,0:T(8,128)S(1)}, f32[1,4,256,512]{3,2,1,0:T(8,128)}, u32[]{:S(2)}) copy-start(f32[1,4,256,512]{3,2,1,0:T(8,128)} %field.1) | copy-start | bytes 6291460

commit v2 on v0

v2 whole, which is shorter than its diff:
```python
import functools

import jax
import jax.numpy as jnp
from jax import lax
from jax.experimental import pallas as pl
from jax.experimental.pallas import tpu as pltpu
from jax.sharding import PartitionSpec as P

STEPS = 4
DT = 0.1
EPS2 = 1.5
PAD = 8
EXT = 8
RUN = 4


def kernel(
    cfg, field, mobility, frac, sides, out,
    phi, mob, zbuf, xbuf, coef,
    ls, cs, cr, h0s, h0r, hs, hr, fs, fr, zs, zr, xs, xr,
):
    images, spaces, planes, ny, nz = cfg
    half = ny // 2
    rows = half + EXT
    unit = half // 2
    chunks = ((0, unit), (unit, rows - unit))
    parts = ((0, unit + 8), (unit + 8, rows - unit - 8))
    first, last = 1, planes
    img = lax.axis_index("image")
    sp = lax.axis_index("space")
    hi = lax.rem(img, 2)
    other = 1 - hi
    z = img // 2
    partner = img + 1 - 2 * hi
    core = lax.rem(sp, 2)
    place = lax.rem(sp, RUN)

    def half_of(which, where):
        return lax.rem(which + lax.rem(where // RUN, 2), 2)

    def base_of(h):
        return pl.multiple_of(h * (half - EXT), 8)

    h = half_of(hi, sp)
    has_l = sp > 0
    has_r = sp < spaces - 1
    in_l = core == 1
    in_r = core == 0
    img_l = 2 * z + jnp.where(place == 0, other, hi)
    img_r = 2 * z + jnp.where(place == RUN - 1, other, hi)
    has_dn = z > 0
    has_up = img < images - 2
    mesh_id = pl.DeviceIdType.MESH

    def cells(t, a, p, r, n):
        return phi.at[t, a, p, pl.ds(PAD + r, n)]

    def edge(side):
        return (last, 0, sp + 1) if side == 0 else (first, planes + 1, sp - 1)

    def halo0(side, tgt):
        p, q, where = edge(side)
        return pltpu.make_async_remote_copy(
            src_ref=field.at[0, p - 1, pl.ds(base_of(half_of(tgt, where)), rows)],
            dst_ref=cells(0, hi, q, 0, rows),
            send_sem=h0s.at[side, tgt],
            recv_sem=h0r.at[side, hi],
            device_id={"image": 2 * z + tgt, "space": where},
            device_id_type=mesh_id,
        )

    def halo_in(side, a):
        p, q, where = edge(side)
        return pltpu.make_async_remote_copy(
            src_ref=cells(0, a, p, 0, rows),
            dst_ref=cells(0, a, q, 0, rows),
            send_sem=h0s.at[side, a],
            recv_sem=h0r.at[side, a],
            device_id={"image": img, "space": where},
            device_id_type=mesh_id,
        )

    def halo(t, side, a, c):
        p, q, where = edge(side)
        r, n = chunks[c]
        return pltpu.make_async_remote_copy(
            src_ref=cells(t, a, p, r, n),
            dst_ref=cells(t, a, q, r, n),
            send_sem=hs.at[t - 1, side, a, c],
            recv_sem=hr.at[t - 1, side, a, c],
            device_id={"image": img_r if side == 0 else img_l, "space": where},
            device_id_type=mesh_id,
        )

    def fcopy(i, p, a):
        r, n = parts[i]
        return pltpu.make_async_remote_copy(
            src_ref=field.at[0, p, pl.ds(base_of(1 - h) + r, n)],
            dst_ref=cells(0, a, p + 1, r, n),
            send_sem=fs.at[i, p],
            recv_sem=fr.at[i, p],
            device_id={"image": partner},
            device_id_type=mesh_id,
        )

    def rows_of(ref, k, p, c):
        return ref.at[k, p, pl.ds(pl.multiple_of(c * unit, 8), unit)]

    def zcopy(a, p, c):
        return pltpu.make_async_remote_copy(
            src_ref=cells(STEPS, a, p + 1, pl.multiple_of(h * EXT + c * unit, 8), unit),
            dst_ref=rows_of(zbuf, 1 - a, p, c),
            send_sem=zs.at[a, p, c],
            recv_sem=zr.at[1 - a, p, c],
            device_id={"image": img - 2 + 4 * a},
            device_id_type=mesh_id,
        )

    def xcopy(p, c, which):
        return pltpu.make_async_remote_copy(
            src_ref=xbuf.at[p, pl.ds(pl.multiple_of(c * unit, 8), unit)],
            dst_ref=out.at[0, p, pl.ds(pl.multiple_of(which * half + c * unit, 8), unit)],
            send_sem=xs.at[p, c],
            recv_sem=xr.at[p, c],
            device_id={"image": partner},
            device_id_type=mesh_id,
        )

    def ccopy(a):
        return pltpu.make_async_remote_copy(
            src_ref=coef.at[a],
            dst_ref=coef.at[a],
            send_sem=cs,
            recv_sem=cr,
            device_id={"image": partner},
            device_id_type=mesh_id,
        )

    def when(flag, *more):
        for item in more:
            flag = jnp.logical_and(flag, item)
        return pl.when(flag)

    def send_halo(t, a, c):
        @when(has_r)
        def _():
            halo(t, 0, a, c).start()

        @when(has_l)
        def _():
            halo(t, 1, a, c).start()

    def wait_halo(t, a, c):
        @when(has_l)
        def _():
            halo(t, 0, a, c).wait_recv()

        @when(has_r)
        def _():
            halo(t, 1, a, c).wait_recv()

    def advance(t, a, p, c):
        r, n = chunks[c]
        lane = lax.broadcasted_iota(jnp.int32, (n, nz), 1)
        here = phi[t, a, p, pl.ds(PAD + r, n)]
        s = phi[t, a, p - 1, pl.ds(PAD + r, n)] + phi[t, a, p + 1, pl.ds(PAD + r, n)]
        wide = phi[t, a, p, pl.ds(PAD + r - 8, n + 16)]
        s = s + wide[7 : 7 + n] + wide[9 : 9 + n]
        s = s + jnp.where(lane == 0, 0.0, pltpu.roll(here, 1, 1))
        s = s + jnp.where(lane == nz - 1, 0.0, pltpu.roll(here, nz - 1, 1))
        m = mob[p - 1, pl.ds(r, n)]
        phi[t + 1, a, p, pl.ds(PAD + r, n)] = here + m * (EPS2 * s - here * (8.0 + here * here))

    inner = tuple(range(first + 1, last))

    loads = [
        pltpu.make_async_copy(field.at[0, p, pl.ds(base_of(h), rows)], cells(0, hi, p + 1, 0, rows), ls.at[p])
        for p in range(planes)
    ]
    loads.append(pltpu.make_async_copy(mobility.at[pl.ds(0, planes), pl.ds(base_of(h), rows)], mob, ls.at[planes]))
    for copy in loads:
        copy.start()

    barrier = pltpu.get_barrier_semaphore()

    def greet(where_img, where_sp):
        pl.semaphore_signal(barrier, 1, device_id={"image": where_img, "space": where_sp}, device_id_type=mesh_id)

    for side, known, inside in ((1, has_l, in_l), (0, has_r, in_r)):
        where = edge(side)[2]

        @when(known, inside)
        def _():
            greet(img, where)

        @when(known, jnp.logical_not(inside))
        def _():
            greet(2 * z, where)
            greet(2 * z + 1, where)

    greet(partner, sp)

    @when(has_dn)
    def _():
        greet(img - 2, sp)

    @when(has_up)
    def _():
        greet(img + 2, sp)

    coef[hi, 0] = jnp.full((8, nz), frac[0], jnp.float32)
    coef[hi, 1] = jnp.full((8, nz), sides[0].astype(jnp.float32), jnp.float32)

    def clear_rows(t, _):
        for a in range(2):
            for p in range(first, last + 1):
                phi[t, a, p, pl.ds(0, PAD)] = jnp.zeros((PAD, nz), jnp.float32)
                phi[t, a, p, pl.ds(PAD + rows, PAD)] = jnp.zeros((PAD, nz), jnp.float32)
        return 0

    lax.fori_loop(0, STEPS, clear_rows, 0)

    def clear_halo(q):
        def body(t, _):
            for a in range(2):
                phi[t, a, q, pl.ds(PAD, rows)] = jnp.zeros((rows, nz), jnp.float32)
            return 0

        lax.fori_loop(0, STEPS, body, 0)

    @when(jnp.logical_not(has_l))
    def _():
        clear_halo(0)

    @when(jnp.logical_not(has_r))
    def _():
        clear_halo(planes + 1)

    for a, known in ((0, has_dn), (1, has_up)):

        @when(jnp.logical_not(known))
        def _():
            def body(p, _):
                zbuf[a, p] = jnp.zeros((half, nz), jnp.float32)
                return 0

            lax.fori_loop(0, planes, body, 0)

    count = lambda flag: jnp.where(flag, 1, 0)
    expect = 1 + count(has_dn) + count(has_up)
    expect = expect + count(has_l) * (2 - count(in_l)) + count(has_r) * (2 - count(in_r))
    pl.semaphore_wait(barrier, expect)

    for side, known, inside in ((0, has_r, in_r), (1, has_l, in_l)):

        @when(known, jnp.logical_not(inside))
        def _():
            for tgt in range(2):
                halo0(side, tgt).start()

    for i in range(len(parts)):
        for p in range(planes):
            fcopy(i, p, hi).start()
    ccopy(hi).start()

    for copy in loads:
        copy.wait()

    def send_in(a):
        for side, known, inside in ((0, has_r, in_r), (1, has_l, in_l)):

            @when(known, inside)
            def _():
                halo_in(side, a).start()

    send_in(hi)

    def scale(p, _):
        mob[p] = DT * mob[p]
        return 0

    lax.fori_loop(0, planes, scale, 0)

    def begin(k, _):
        a = lax.rem(hi + k, 2)

        @when(k == 1)
        def _():
            for i in range(len(parts)):
                for p in range(planes):
                    fcopy(i, p, other).wait_recv()
            send_in(other)

        for c in range(len(chunks)):
            for p in inner:
                advance(0, a, p, c)

        @when(has_l)
        def _():
            halo_in(0, a).wait_recv()

        @when(has_r)
        def _():
            halo_in(1, a).wait_recv()

        for c in range(len(chunks)):
            advance(0, a, first, c)
            advance(0, a, last, c)
            send_halo(1, a, c)
        return 0

    lax.fori_loop(0, 2, begin, 0)

    def step(t, _):
        def within(k, _):
            a = lax.rem(hi + k, 2)
            for c in range(len(chunks)):
                for p in inner:
                    advance(t, a, p, c)
            return 0

        lax.fori_loop(0, 2, within, 0)

        def rim(k, _):
            a = lax.rem(hi + k, 2)
            for c in range(len(chunks)):
                wait_halo(t, a, c)
                advance(t, a, first, c)
                advance(t, a, last, c)
                send_halo(t + 1, a, c)
            return 0

        lax.fori_loop(0, 2, rim, 0)
        return 0

    lax.fori_loop(1, STEPS - 1, step, 0)

    end = STEPS - 1

    def known_z(a):
        return jnp.logical_and(img - 2 + 4 * a >= 0, img - 2 + 4 * a < images)

    def final_within(k, _):
        a = lax.rem(hi + k, 2)
        for c in range(len(chunks)):
            for p in inner:
                advance(end, a, p, c)

        @when(known_z(a))
        def _():
            for p in inner:
                for c in range(2):
                    zcopy(a, p - 1, c).start()

        return 0

    lax.fori_loop(0, 2, final_within, 0)

    def final_rim(k, _):
        a = lax.rem(hi + k, 2)
        for c in range(len(chunks)):
            wait_halo(end, a, c)
            advance(end, a, first, c)
            advance(end, a, last, c)

        @when(known_z(a))
        def _():
            for p in (first, last):
                for c in range(2):
                    zcopy(a, p - 1, c).start()

        return 0

    lax.fori_loop(0, 2, final_rim, 0)
    ccopy(other).wait_recv()

    def mix(a, p, c):
        at = pl.ds(pl.multiple_of(PAD + h * EXT + c * unit, 8), unit)
        mine = phi[STEPS, a, p + 1, at]
        beside = phi[STEPS, 1 - a, p + 1, at]
        along = zbuf[a, p, pl.ds(pl.multiple_of(c * unit, 8), unit)]
        f = coef[a, 0, pl.ds(0, 1)]
        side = coef[a, 1, pl.ds(0, 1)]
        use_z = jnp.broadcast_to(side, (unit, nz)) == a.astype(jnp.float32)
        return mine + f * (jnp.where(use_z, along, beside) - mine)

    def blend(u, _):
        v = lax.rem(u, 4)
        c = lax.rem(v, 2)
        p = jnp.where(u < 4, 1 + v // 2, 3 * (v // 2))
        for a, known in ((0, has_dn), (1, has_up)):

            @when(known)
            def _():
                zcopy(1 - a, p, c).wait_recv()

        xbuf[p, pl.ds(pl.multiple_of(c * unit, 8), unit)] = mix(other, p, c)
        out[0, p, pl.ds(pl.multiple_of(h * half + c * unit, 8), unit)] = mix(hi, p, c)
        xcopy(p, c, h).start()
        return 0

    lax.fori_loop(0, planes * 2, blend, 0)

    for side, known in ((0, has_r), (1, has_l)):

        @when(known)
        def _():
            for a in range(2):
                halo_in(side, a).wait_send()

            def body(i, _):
                for a in range(2):
                    for c in range(len(chunks)):
                        halo(i, side, a, c).wait_send()
                return 0

            lax.fori_loop(1, STEPS, body, 0)

    for i in range(len(parts)):
        for p in range(planes):
            fcopy(i, p, hi).wait_send()
    ccopy(hi).wait_send()

    def drain(u, _):
        p, c = u // 2, lax.rem(u, 2)
        for a, known in ((0, has_dn), (1, has_up)):

            @when(known)
            def _():
                zcopy(a, p, c).wait_send()

        xcopy(p, c, h).wait_send()
        xcopy(p, c, 1 - h).wait_recv()
        return 0

    lax.fori_loop(0, planes * 2, drain, 0)


def local(images, spaces, field, mobility, fractions, sides):
    _, planes, ny, nz = field.shape
    half = ny // 2
    dma = pltpu.SemaphoreType.DMA
    return pl.pallas_call(
        functools.partial(kernel, (images, spaces, planes, ny, nz)),
        out_shape=jax.ShapeDtypeStruct(field.shape, jnp.float32),
        in_specs=[
            pl.BlockSpec(memory_space=pltpu.HBM),
            pl.BlockSpec(memory_space=pltpu.HBM),
            pl.BlockSpec(memory_space=pltpu.SMEM),
            pl.BlockSpec(memory_space=pltpu.SMEM),
        ],
        out_specs=pl.BlockSpec(memory_space=pltpu.VMEM),
        scratch_shapes=[
            pltpu.VMEM((STEPS + 1, 2, planes + 2, half + EXT + 2 * PAD, nz), jnp.float32),
            pltpu.VMEM((planes, half + EXT, nz), jnp.float32),
            pltpu.VMEM((2, planes, half, nz), jnp.float32),
            pltpu.VMEM((planes, half, nz), jnp.float32),
            pltpu.VMEM((2, 2, 8, nz), jnp.float32),
            dma((planes + 1,)),
            dma,
            dma,
            dma((2, 2)),
            dma((2, 2)),
            dma((STEPS - 1, 2, 2, 2)),
            dma((STEPS - 1, 2, 2, 2)),
            dma((2, planes)),
            dma((2, planes)),
            dma((2, planes, 2)),
            dma((2, planes, 2)),
            dma((planes, 2)),
            dma((planes, 2)),
        ],
        compiler_params=pltpu.CompilerParams(
            collective_id=0, has_side_effects=True, vmem_limit_bytes=50 * 1024 * 1024
        ),
    )(field, mobility, fractions, sides)


def solution(mesh):
    return jax.shard_map(
        functools.partial(local, mesh.shape["image"], mesh.shape["space"]),
        mesh=mesh,
        in_specs=(P("image", "space", None, None), P("space", None, None), P("image"), P("image")),
        out_specs=P("image", "space", None, None),
        check_vma=False,
    )
```

time: 182 us -> 93 us (0.51)
  the two profiles are of different devices: /device:TPU:237 before, /device:TPU:219 now
where the time goes in v2:
time: 93 us; the launch traced here: 92.8 us
  Pallas kernels  90.2 us (97%)
  local copies, waits for them, and re-layouts  1.32 us (1%)
  between operations  1.3 us (1%)
    pallas_call x1, Pallas kernels, local(): pl.pallas_call(functools.partial(kernel, (images, spaces, planes, ny, nz)...  90.2 us

profile of v2, /device:TPU:219, one launch (start us, length us, event | category | flops | bytes accessed | tf_op | source)
XLA Modules:
  0.0 92.8 jit_solution(6066861103875333305)
XLA Ops:
  1.3 90.2 %shard_map.46 = f32[1,4,256,512]{3,2,1,0:T(8,128)S(1)} custom-call(f32[1,4,256,512]{3,2,1,0:T(8,128)} %field.1, f32[4,256,512]{2,1,0:T(8,128)} %mobility.1, f32[1]{0:T(128)S(6)} %copy.6.frac, s32[1]{0:T(128)S(6)} %copy.7.sides), custom_call_target="tpu_custom_call" | custom-call | tf_op jit(solution)/shard_map/pallas_call | solution.py:444
  91.5 1.3 %copy.8 = f32[1,4,256,512]{3,2,1,0:T(8,128)} copy(f32[1,4,256,512]{3,2,1,0:T(8,128)S(1)} %shard_map.46) | data formatting | bytes 4194304

commit v3 on v2

v3 whole, which is shorter than its diff:
```python
import functools

import jax
import jax.numpy as jnp
from jax import lax
from jax.experimental import pallas as pl
from jax.experimental.pallas import tpu as pltpu
from jax.sharding import PartitionSpec as P

STEPS = 4
DT = 0.1
EPS2 = 1.5
PAD = 8
EXT = 8
CHUNKS = 4
RUN = 4


def kernel(
    cfg, field, mobility, frac, sides, out,
    phi, mob, zbuf, xbuf, coef,
    ls, cs, cr, h0s, h0r, hs, hr, fs, fr, zs, zr, xs, xr,
):
    images, spaces, planes, ny, nz = cfg
    half = ny // 2
    rows = half + EXT
    unit = half // CHUNKS
    first, last = 1, planes
    inner = tuple(range(first + 1, last))
    img = lax.axis_index("image")
    sp = lax.axis_index("space")
    hi = lax.rem(img, 2)
    other = 1 - hi
    z = img // 2
    partner = img + 1 - 2 * hi
    core = lax.rem(sp, 2)
    place = lax.rem(sp, RUN)

    def bound(c, t):
        if c == 0:
            return 0
        if c == CHUNKS:
            return rows
        return c * unit + 8 * STEPS - 8 * t

    def span(c, t):
        return bound(c, t), bound(c + 1, t) - bound(c, t)

    def part(c):
        lo = 0 if c == 0 else min(bound(c, 0) + 8, rows)
        return lo, min(bound(c + 1, 0) + 8, rows) - lo

    def half_of(which, where):
        return lax.rem(which + lax.rem(where // RUN, 2), 2)

    def base_of(h):
        return pl.multiple_of(h * (half - EXT), 8)

    h = half_of(hi, sp)
    has_l = sp > 0
    has_r = sp < spaces - 1
    in_l = core == 1
    in_r = core == 0
    img_l = 2 * z + jnp.where(place == 0, other, hi)
    img_r = 2 * z + jnp.where(place == RUN - 1, other, hi)
    has_dn = z > 0
    has_up = img < images - 2
    mesh_id = pl.DeviceIdType.MESH

    def cells(t, a, p, r, n):
        return phi.at[t, a, p, pl.ds(PAD + r, n)]

    def edge(side):
        return (last, 0, sp + 1) if side == 0 else (first, planes + 1, sp - 1)

    def halo0(side, tgt, c):
        p, q, where = edge(side)
        r, n = span(c, 0)
        return pltpu.make_async_remote_copy(
            src_ref=field.at[0, p - 1, pl.ds(base_of(half_of(tgt, where)) + r, n)],
            dst_ref=cells(0, hi, q, r, n),
            send_sem=h0s.at[side, tgt, c],
            recv_sem=h0r.at[side, hi, c],
            device_id={"image": 2 * z + tgt, "space": where},
            device_id_type=mesh_id,
        )

    def halo_in(side, a, c):
        p, q, where = edge(side)
        r, n = span(c, 0)
        return pltpu.make_async_remote_copy(
            src_ref=cells(0, a, p, r, n),
            dst_ref=cells(0, a, q, r, n),
            send_sem=h0s.at[side, a, c],
            recv_sem=h0r.at[side, a, c],
            device_id={"image": img, "space": where},
            device_id_type=mesh_id,
        )

    def halo(t, side, a, c):
        if t == 0:
            return halo_in(side, a, c)
        p, q, where = edge(side)
        r, n = span(c, t)
        return pltpu.make_async_remote_copy(
            src_ref=cells(t, a, p, r, n),
            dst_ref=cells(t, a, q, r, n),
            send_sem=hs.at[t - 1, side, a, c],
            recv_sem=hr.at[t - 1, side, a, c],
            device_id={"image": img_r if side == 0 else img_l, "space": where},
            device_id_type=mesh_id,
        )

    def fcopy(c, p, a):
        r, n = part(c)
        return pltpu.make_async_remote_copy(
            src_ref=field.at[0, p, pl.ds(base_of(1 - h) + r, n)],
            dst_ref=cells(0, a, p + 1, r, n),
            send_sem=fs.at[c, p],
            recv_sem=fr.at[c, p],
            device_id={"image": partner},
            device_id_type=mesh_id,
        )

    def zcopy(a, p, c):
        return pltpu.make_async_remote_copy(
            src_ref=cells(STEPS, a, p + 1, pl.multiple_of(h * EXT + c * unit, 8), unit),
            dst_ref=zbuf.at[1 - a, p, pl.ds(c * unit, unit)],
            send_sem=zs.at[a, p, c],
            recv_sem=zr.at[1 - a, p, c],
            device_id={"image": img - 2 + 4 * a},
            device_id_type=mesh_id,
        )

    def xcopy(p, c, which):
        return pltpu.make_async_remote_copy(
            src_ref=xbuf.at[p, pl.ds(c * unit, unit)],
            dst_ref=out.at[0, p, pl.ds(pl.multiple_of(which * half + c * unit, 8), unit)],
            send_sem=xs.at[p, c],
            recv_sem=xr.at[p, c],
            device_id={"image": partner},
            device_id_type=mesh_id,
        )

    def ccopy(a):
        return pltpu.make_async_remote_copy(
            src_ref=coef.at[a],
            dst_ref=coef.at[a],
            send_sem=cs,
            recv_sem=cr,
            device_id={"image": partner},
            device_id_type=mesh_id,
        )

    def when(flag, *more):
        for item in more:
            flag = jnp.logical_and(flag, item)
        return pl.when(flag)

    def twice(body):
        def one(k, _):
            body(k, lax.rem(hi + k, 2))
            return 0

        lax.fori_loop(0, 2, one, 0)

    def send_halo(t, a, c):
        @when(has_r)
        def _():
            halo(t, 0, a, c).start()

        @when(has_l)
        def _():
            halo(t, 1, a, c).start()

    def wait_halo(t, a, c):
        @when(has_l)
        def _():
            halo(t, 0, a, c).wait_recv()

        @when(has_r)
        def _():
            halo(t, 1, a, c).wait_recv()

    def send_in(a, c):
        for side, known, inside in ((0, has_r, in_r), (1, has_l, in_l)):

            @when(known, inside)
            def _():
                halo_in(side, a, c).start()

    def advance(t, a, p, r, n):
        lane = lax.broadcasted_iota(jnp.int32, (n, nz), 1)
        here = phi[t, a, p, pl.ds(PAD + r, n)]
        s = phi[t, a, p - 1, pl.ds(PAD + r, n)] + phi[t, a, p + 1, pl.ds(PAD + r, n)]
        wide = phi[t, a, p, pl.ds(PAD + r - 8, n + 16)]
        s = s + wide[7 : 7 + n] + wide[9 : 9 + n]
        s = s + jnp.where(lane == 0, 0.0, pltpu.roll(here, 1, 1))
        s = s + jnp.where(lane == nz - 1, 0.0, pltpu.roll(here, nz - 1, 1))
        m = mob[p - 1, pl.ds(r, n)]
        phi[t + 1, a, p, pl.ds(PAD + r, n)] = here + m * (EPS2 * s - here * (8.0 + here * here))

    loads = [
        pltpu.make_async_copy(field.at[0, p, pl.ds(base_of(h), rows)], cells(0, hi, p + 1, 0, rows), ls.at[p])
        for p in range(planes)
    ]
    loads.append(pltpu.make_async_copy(mobility.at[pl.ds(0, planes), pl.ds(base_of(h), rows)], mob, ls.at[planes]))
    for copy in loads:
        copy.start()

    barrier = pltpu.get_barrier_semaphore()

    def greet(where_img, where_sp):
        pl.semaphore_signal(barrier, 1, device_id={"image": where_img, "space": where_sp}, device_id_type=mesh_id)

    for side, known, inside in ((1, has_l, in_l), (0, has_r, in_r)):
        where = edge(side)[2]

        @when(known, inside)
        def _():
            greet(img, where)

        @when(known, jnp.logical_not(inside))
        def _():
            greet(2 * z, where)
            greet(2 * z + 1, where)

    greet(partner, sp)

    @when(has_dn)
    def _():
        greet(img - 2, sp)

    @when(has_up)
    def _():
        greet(img + 2, sp)

    coef[hi, 0] = jnp.full((8, nz), frac[0], jnp.float32)
    coef[hi, 1] = jnp.full((8, nz), sides[0].astype(jnp.float32), jnp.float32)

    def clear_rows(t, _):
        for a in range(2):
            for p in range(first, last + 1):
                phi[t, a, p, pl.ds(0, PAD)] = jnp.zeros((PAD, nz), jnp.float32)
                phi[t, a, p, pl.ds(PAD + rows, PAD)] = jnp.zeros((PAD, nz), jnp.float32)
        return 0

    lax.fori_loop(0, STEPS, clear_rows, 0)

    def clear_halo(q):
        def body(t, _):
            for a in range(2):
                phi[t, a, q, pl.ds(PAD, rows)] = jnp.zeros((rows, nz), jnp.float32)
            return 0

        lax.fori_loop(0, STEPS, body, 0)

    @when(jnp.logical_not(has_l))
    def _():
        clear_halo(0)

    @when(jnp.logical_not(has_r))
    def _():
        clear_halo(planes + 1)

    for a, known in ((0, has_dn), (1, has_up)):

        @when(jnp.logical_not(known))
        def _():
            def body(p, _):
                zbuf[a, p] = jnp.zeros((half, nz), jnp.float32)
                return 0

            lax.fori_loop(0, planes, body, 0)

    count = lambda flag: jnp.where(flag, 1, 0)
    expect = 1 + count(has_dn) + count(has_up)
    expect = expect + count(has_l) * (2 - count(in_l)) + count(has_r) * (2 - count(in_r))
    pl.semaphore_wait(barrier, expect)

    def issue(c):
        for side, known, inside in ((0, has_r, in_r), (1, has_l, in_l)):

            @when(known, jnp.logical_not(inside))
            def _():
                for tgt in range(2):
                    halo0(side, tgt, c).start()

        if part(c)[1] > 0:
            for p in range(planes):
                fcopy(c, p, hi).start()

    issue(0)
    ccopy(hi).start()
    issue(1)
    for copy in loads:
        copy.wait()
    for c in range(CHUNKS):
        send_in(hi, c)

    def scale(p, _):
        mob[p] = DT * mob[p]
        return 0

    lax.fori_loop(0, planes, scale, 0)

    end = STEPS - 1

    def task(c, t):
        r, n = span(c, t)

        def within(k, a):
            if t == 0:

                @when(k == 1)
                def _():
                    if part(c)[1] > 0:
                        for p in range(planes):
                            fcopy(c, p, other).wait_recv()
                    send_in(other, c)

            for p in inner:
                advance(t, a, p, r, n)

        def rim(k, a):
            wait_halo(t, a, c)
            advance(t, a, first, r, n)
            advance(t, a, last, r, n)
            if t < end:
                send_halo(t + 1, a, c)

        if t == 0:

            def both(k, a):
                within(k, a)
                rim(k, a)

            twice(both)
        else:
            twice(within)
            twice(rim)

    def send_z(c):
        for a, known in ((0, has_dn), (1, has_up)):

            @when(known)
            def _():
                for p in (*(q - 1 for q in inner), first - 1, last - 1):
                    zcopy(a, p, c).start()

    def mix(a, p, c):
        mine = phi[STEPS, a, p + 1, pl.ds(pl.multiple_of(PAD + h * EXT + c * unit, 8), unit)]
        beside = phi[STEPS, 1 - a, p + 1, pl.ds(pl.multiple_of(PAD + h * EXT + c * unit, 8), unit)]
        along = zbuf[a, p, pl.ds(c * unit, unit)]
        f = coef[a, 0, pl.ds(0, 1)]
        side = coef[a, 1, pl.ds(0, 1)]
        use_z = jnp.broadcast_to(side, (unit, nz)) == a.astype(jnp.float32)
        return mine + f * (jnp.where(use_z, along, beside) - mine)

    def blend(c):
        if c == 0:
            ccopy(other).wait_recv()

        def body(i, _):
            p = jnp.where(i < planes - 2, i + 1, (planes - 1) * (i - planes + 2))
            for a, known in ((0, has_dn), (1, has_up)):

                @when(known)
                def _():
                    zcopy(1 - a, p, c).wait_recv()

            xbuf[p, pl.ds(c * unit, unit)] = mix(other, p, c)
            out[0, p, pl.ds(pl.multiple_of(h * half + c * unit, 8), unit)] = mix(hi, p, c)
            xcopy(p, c, h).start()
            return 0

        lax.fori_loop(0, planes, body, 0)

    for wave in range(CHUNKS + STEPS - 1):
        for c in range(CHUNKS):
            t = wave - c
            if 0 <= t < STEPS:
                task(c, t)
                if t == 0 and c + 2 < CHUNKS:
                    issue(c + 2)
                if t == end:
                    send_z(c)
        if wave >= STEPS:
            blend(wave - STEPS)
    blend(CHUNKS - 1)

    for side, known in ((0, has_r), (1, has_l)):

        @when(known)
        def _():
            for t in range(STEPS):
                for c in range(CHUNKS):
                    for a in range(2):
                        halo(t, side, a, c).wait_send()

    for c in range(CHUNKS):
        if part(c)[1] > 0:
            for p in range(planes):
                fcopy(c, p, hi).wait_send()
    ccopy(hi).wait_send()

    def drain(p, _):
        for c in range(CHUNKS):
            for a, known in ((0, has_dn), (1, has_up)):

                @when(known)
                def _():
                    zcopy(a, p, c).wait_send()

            xcopy(p, c, h).wait_send()
            xcopy(p, c, 1 - h).wait_recv()
        return 0

    lax.fori_loop(0, planes, drain, 0)


def local(images, spaces, field, mobility, fractions, sides):
    _, planes, ny, nz = field.shape
    half = ny // 2
    dma = pltpu.SemaphoreType.DMA
    return pl.pallas_call(
        functools.partial(kernel, (images, spaces, planes, ny, nz)),
        out_shape=jax.ShapeDtypeStruct(field.shape, jnp.float32),
        in_specs=[
            pl.BlockSpec(memory_space=pltpu.HBM),
            pl.BlockSpec(memory_space=pltpu.HBM),
            pl.BlockSpec(memory_space=pltpu.SMEM),
            pl.BlockSpec(memory_space=pltpu.SMEM),
        ],
        out_specs=pl.BlockSpec(memory_space=pltpu.VMEM),
        scratch_shapes=[
            pltpu.VMEM((STEPS + 1, 2, planes + 2, half + EXT + 2 * PAD, nz), jnp.float32),
            pltpu.VMEM((planes, half + EXT, nz), jnp.float32),
            pltpu.VMEM((2, planes, half, nz), jnp.float32),
            pltpu.VMEM((planes, half, nz), jnp.float32),
            pltpu.VMEM((2, 2, 8, nz), jnp.float32),
            dma((planes + 1,)),
            dma,
            dma,
            dma((2, 2, CHUNKS)),
            dma((2, 2, CHUNKS)),
            dma((STEPS - 1, 2, 2, CHUNKS)),
            dma((STEPS - 1, 2, 2, CHUNKS)),
            dma((CHUNKS, planes)),
            dma((CHUNKS, planes)),
            dma((2, planes, CHUNKS)),
            dma((2, planes, CHUNKS)),
            dma((planes, CHUNKS)),
            dma((planes, CHUNKS)),
        ],
        compiler_params=pltpu.CompilerParams(
            collective_id=0, has_side_effects=True, vmem_limit_bytes=50 * 1024 * 1024
        ),
    )(field, mobility, fractions, sides)


def solution(mesh):
    return jax.shard_map(
        functools.partial(local, mesh.shape["image"], mesh.shape["space"]),
        mesh=mesh,
        in_specs=(P("image", "space", None, None), P("space", None, None), P("image"), P("image")),
        out_specs=P("image", "space", None, None),
        check_vma=False,
    )
```

time: 93 us -> 97.7 us (1.051)
  the two profiles are of different devices: /device:TPU:219 before, /device:TPU:206 now
where the time goes in v3:
time: 97.7 us; the launch traced here: 97.5 us
  Pallas kernels  94.9 us (97%)
  local copies, waits for them, and re-layouts  1.32 us (1%)
  between operations  1.3 us (1%)
    pallas_call x1, Pallas kernels, local(): pl.pallas_call(functools.partial(kernel, (images, spaces, planes, ny, nz)...  94.9 us

profile of v3, /device:TPU:206, one launch (start us, length us, event | category | flops | bytes accessed | tf_op | source)
XLA Modules:
  0.0 97.5 jit_solution(1360062158790053301)
XLA Ops:
  1.3 94.9 %shard_map.46 = f32[1,4,256,512]{3,2,1,0:T(8,128)S(1)} custom-call(f32[1,4,256,512]{3,2,1,0:T(8,128)} %field.1, f32[4,256,512]{2,1,0:T(8,128)} %mobility.1, f32[1]{0:T(128)S(6)} %copy.6.frac, s32[1]{0:T(128)S(6)} %copy.7.sides), custom_call_target="tpu_custom_call" | custom-call | tf_op jit(solution)/shard_map/pallas_call | solution.py:426
  96.2 1.3 %copy.8 = f32[1,4,256,512]{3,2,1,0:T(8,128)} copy(f32[1,4,256,512]{3,2,1,0:T(8,128)S(1)} %shard_map.46) | data formatting | bytes 4194304

commit v4 on v0

v4 whole, which is shorter than its diff:
```python
import functools

import jax
import jax.numpy as jnp
from jax import lax
from jax.experimental import pallas as pl
from jax.experimental.pallas import tpu as pltpu
from jax.sharding import PartitionSpec as P

STEPS = 4
DT = 0.1
EPS2 = 1.5
PAD = 8
EXT = 8
RUN = 4


def kernel(
    cfg, field, mobility, frac, sides, out,
    phi, mob, zbuf, xbuf, coef,
    ls, cs, cr, h0s, h0r, hs, hr, ns, nr, fs, fr, zs, zr, xs, xr,
):
    images, spaces, planes, ny, nz = cfg
    half = ny // 2
    rows = half + EXT
    unit = half // 2
    chunks = ((0, unit), (unit, rows - unit))
    img = lax.axis_index("image")
    sp = lax.axis_index("space")
    hi = lax.rem(img, 2)
    other = 1 - hi
    z = img // 2
    partner = img + 1 - 2 * hi
    core = lax.rem(sp, 2)
    place = lax.rem(sp, RUN)
    mesh_id = pl.DeviceIdType.MESH

    def half_of(which, where):
        return lax.rem(which + lax.rem(where // RUN, 2), 2)

    def base_of(h):
        return pl.multiple_of(h * (half - EXT), 8)

    h = half_of(hi, sp)
    has_dn = z > 0
    has_up = img < images - 2

    sp_e = sp - 1 + 2 * core
    sp_n = sp + 1 - 2 * core
    has_e = jnp.logical_and(sp_e >= 0, sp_e < spaces)
    crosses = place == core * (RUN - 1)
    img_e = 2 * z + jnp.where(crosses, other, hi)
    slot_e = core * (planes + 1)
    slot_n = (1 - core) * (planes + 1)

    def at(d):
        return core * planes + (1 - 2 * core) * (d + 1) + core

    def cells(t, a, p, r, n):
        return phi.at[t, a, p, pl.ds(PAD + r, n)]

    def halo0(tgt):
        return pltpu.make_async_remote_copy(
            src_ref=field.at[0, at(0) - 1, pl.ds(base_of(half_of(tgt, sp_e)), rows)],
            dst_ref=cells(0, hi, slot_n, 0, rows),
            send_sem=h0s.at[tgt],
            recv_sem=h0r.at[hi],
            device_id={"image": 2 * z + tgt, "space": sp_e},
            device_id_type=mesh_id,
        )

    def halo0_in(a):
        return pltpu.make_async_remote_copy(
            src_ref=cells(0, a, at(0), 0, rows),
            dst_ref=cells(0, a, slot_e, 0, rows),
            send_sem=h0s.at[a],
            recv_sem=h0r.at[a],
            device_id={"image": img_e, "space": sp_e},
            device_id_type=mesh_id,
        )

    def halo(t, a, c, arriving=False):
        r, n = chunks[c]
        return pltpu.make_async_remote_copy(
            src_ref=cells(t, a, at(0), r, n),
            dst_ref=cells(t, a, slot_e if arriving else slot_n, r, n),
            send_sem=hs.at[t - 1, a, c],
            recv_sem=hr.at[t - 1, a, c],
            device_id={"image": img_e, "space": sp_e},
            device_id_type=mesh_id,
        )

    def near(t, a, arriving=False):
        return pltpu.make_async_remote_copy(
            src_ref=cells(t, a, at(planes - 1), 0, rows),
            dst_ref=cells(t, a, slot_n if arriving else slot_e, 0, rows),
            send_sem=ns.at[t, a],
            recv_sem=nr.at[t, a],
            device_id={"space": sp_n},
            device_id_type=mesh_id,
        )

    def fcopy(d, a):
        return pltpu.make_async_remote_copy(
            src_ref=field.at[0, at(d) - 1, pl.ds(base_of(1 - h), rows)],
            dst_ref=cells(0, a, at(d), 0, rows),
            send_sem=fs.at[d],
            recv_sem=fr.at[d],
            device_id={"image": partner},
            device_id_type=mesh_id,
        )

    def zcopy(a, d, c):
        return pltpu.make_async_remote_copy(
            src_ref=cells(STEPS, a, at(d), pl.multiple_of(h * EXT + c * unit, 8), unit),
            dst_ref=zbuf.at[1 - a, d, pl.ds(c * unit, unit)],
            send_sem=zs.at[a, d, c],
            recv_sem=zr.at[1 - a, d, c],
            device_id={"image": img - 2 + 4 * a},
            device_id_type=mesh_id,
        )

    def xcopy(d, c, which):
        return pltpu.make_async_remote_copy(
            src_ref=xbuf.at[d, pl.ds(c * unit, unit)],
            dst_ref=out.at[0, at(d) - 1, pl.ds(pl.multiple_of(which * half + c * unit, 8), unit)],
            send_sem=xs.at[d, c],
            recv_sem=xr.at[d, c],
            device_id={"image": partner},
            device_id_type=mesh_id,
        )

    def ccopy(a):
        return pltpu.make_async_remote_copy(
            src_ref=coef.at[a],
            dst_ref=coef.at[a],
            send_sem=cs,
            recv_sem=cr,
            device_id={"image": partner},
            device_id_type=mesh_id,
        )

    def when(flag, *more):
        for item in more:
            flag = jnp.logical_and(flag, item)
        return pl.when(flag)

    def loop(lo, hi_, body):
        def one(i, _):
            body(i)
            return 0

        lax.fori_loop(lo, hi_, one, 0)

    def twice(body):
        loop(0, 2, lambda k: body(k, lax.rem(hi + k, 2)))

    def advance(t, a, d, r, n):
        p = at(d)
        lane = lax.broadcasted_iota(jnp.int32, (n, nz), 1)
        here = phi[t, a, p, pl.ds(PAD + r, n)]
        s = phi[t, a, p - 1, pl.ds(PAD + r, n)] + phi[t, a, p + 1, pl.ds(PAD + r, n)]
        wide = phi[t, a, p, pl.ds(PAD + r - 8, n + 16)]
        s = s + wide[7 : 7 + n] + wide[9 : 9 + n]
        s = s + jnp.where(lane == 0, 0.0, pltpu.roll(here, 1, 1))
        s = s + jnp.where(lane == nz - 1, 0.0, pltpu.roll(here, nz - 1, 1))
        m = mob[p - 1, pl.ds(r, n)]
        phi[t + 1, a, p, pl.ds(PAD + r, n)] = here + m * (EPS2 * s - here * (8.0 + here * here))

    def whole(t, a, d):
        advance(t, a, d, 0, rows)

    loads = [
        pltpu.make_async_copy(field.at[0, p, pl.ds(base_of(h), rows)], cells(0, hi, p + 1, 0, rows), ls.at[p])
        for p in range(planes)
    ]
    loads.append(pltpu.make_async_copy(mobility.at[pl.ds(0, planes), pl.ds(base_of(h), rows)], mob, ls.at[planes]))
    for copy in loads:
        copy.start()

    barrier = pltpu.get_barrier_semaphore()

    def greet(where_img, where_sp):
        pl.semaphore_signal(barrier, 1, device_id={"image": where_img, "space": where_sp}, device_id_type=mesh_id)

    @when(has_e)
    def _():
        greet(2 * z, sp_e)
        greet(2 * z + 1, sp_e)

    greet(partner, sp)
    greet(img, sp_n)

    @when(has_dn)
    def _():
        greet(img - 2, sp)

    @when(has_up)
    def _():
        greet(img + 2, sp)

    coef[hi, 0] = jnp.full((8, nz), frac[0], jnp.float32)
    coef[hi, 1] = jnp.full((8, nz), sides[0].astype(jnp.float32), jnp.float32)

    def clear_rows(t):
        for a in range(2):
            for p in range(1, planes + 1):
                phi[t, a, p, pl.ds(0, PAD)] = jnp.zeros((PAD, nz), jnp.float32)
                phi[t, a, p, pl.ds(PAD + rows, PAD)] = jnp.zeros((PAD, nz), jnp.float32)

    loop(0, STEPS, clear_rows)

    @when(jnp.logical_not(has_e))
    def _():
        def body(t):
            for a in range(2):
                phi[t, a, slot_e, pl.ds(PAD, rows)] = jnp.zeros((rows, nz), jnp.float32)

        loop(0, STEPS, body)

    for a, known in ((0, has_dn), (1, has_up)):

        @when(jnp.logical_not(known))
        def _():
            def body(d):
                zbuf[a, d] = jnp.zeros((half, nz), jnp.float32)

            loop(0, planes, body)

    count = lambda flag: jnp.where(flag, 1, 0)
    pl.semaphore_wait(barrier, 2 + count(has_dn) + count(has_up) + 2 * count(has_e))

    @when(has_e)
    def _():
        for tgt in range(2):
            halo0(tgt).start()

    early = planes // 2
    for d in range(early):
        fcopy(d, hi).start()
    ccopy(hi).start()
    for copy in loads:
        copy.wait()
    near(0, hi).start()

    def scale(p):
        mob[p] = DT * mob[p]

    loop(0, planes, scale)

    def send_z(a, d):
        @when(img - 2 + 4 * a >= 0, img - 2 + 4 * a < images)
        def _():
            for c in range(2):
                zcopy(a, d, c).start()

    def begin(k, a):
        @when(k == 1)
        def _():
            for d in range(early):
                fcopy(d, other).wait_recv()

        @when(has_e)
        def _():
            halo0_in(a).wait_recv()

        for c in range(len(chunks)):
            advance(0, a, 0, *chunks[c])

            @when(has_e)
            def _():
                halo(1, a, c).start()

        @when(k == 0)
        def _():
            for d in range(early, planes):
                fcopy(d, hi).start()

        @when(k == 1)
        def _():
            for d in range(early, planes):
                fcopy(d, other).wait_recv()
            near(0, other).start()

        def deeper(t):
            near(t, a, True).wait_recv()
            whole(t, a, planes - 1)

            @when(t < STEPS - 1)
            def _():
                near(t + 1, a).start()

            loop(0, planes - 1 - jnp.maximum(t, 1), lambda i: whole(t, a, planes - 2 - i))

        loop(0, STEPS, deeper)
        send_z(a, planes - 1)

    twice(begin)

    def mix(a, d, c):
        p = at(d)
        here = pl.ds(pl.multiple_of(PAD + h * EXT + c * unit, 8), unit)
        mine = phi[STEPS, a, p, here]
        beside = phi[STEPS, 1 - a, p, here]
        along = zbuf[a, d, pl.ds(c * unit, unit)]
        f = coef[a, 0, pl.ds(0, 1)]
        side = coef[a, 1, pl.ds(0, 1)]
        use_z = jnp.broadcast_to(side, (unit, nz)) == a.astype(jnp.float32)
        return mine + f * (jnp.where(use_z, along, beside) - mine)

    def blend(d):
        for c in range(2):
            for a, known in ((0, has_dn), (1, has_up)):

                @when(known)
                def _():
                    zcopy(1 - a, d, c).wait_recv()

            xbuf[d, pl.ds(c * unit, unit)] = mix(other, d, c)
            out[0, at(d) - 1, pl.ds(pl.multiple_of(h * half + c * unit, 8), unit)] = mix(hi, d, c)
            xcopy(d, c, h).start()

    ccopy(other).wait_recv()

    def extend(r):
        def face(k, a):
            for c in range(len(chunks)):

                @when(has_e)
                def _():
                    halo(r, a, c, True).wait_recv()

                advance(r, a, 0, *chunks[c])

                @when(has_e, r < STEPS - 1)
                def _():
                    halo(r + 1, a, c).start()

        twice(face)

        def behind(k, a):
            loop(1, STEPS - r, lambda j: whole(r + j, a, j))
            send_z(a, STEPS - 1 - r)

        twice(behind)
        blend(STEPS - r)

    loop(1, STEPS, extend)
    blend(0)

    @when(has_e)
    def _():
        for tgt in range(2):
            halo0(tgt).wait_send()

        def body(t):
            for a in range(2):
                for c in range(len(chunks)):
                    halo(t, a, c).wait_send()

        loop(1, STEPS, body)

    def sent(t):
        for a in range(2):
            near(t, a).wait_send()

    loop(0, STEPS, sent)
    ccopy(hi).wait_send()

    def drain(d):
        fcopy(d, hi).wait_send()
        for c in range(2):
            for a, known in ((0, has_dn), (1, has_up)):

                @when(known)
                def _():
                    zcopy(a, d, c).wait_send()

            xcopy(d, c, h).wait_send()
            xcopy(d, c, 1 - h).wait_recv()

    loop(0, planes, drain)


def local(images, spaces, field, mobility, fractions, sides):
    _, planes, ny, nz = field.shape
    half = ny // 2
    dma = pltpu.SemaphoreType.DMA
    return pl.pallas_call(
        functools.partial(kernel, (images, spaces, planes, ny, nz)),
        out_shape=jax.ShapeDtypeStruct(field.shape, jnp.float32),
        in_specs=[
            pl.BlockSpec(memory_space=pltpu.HBM),
            pl.BlockSpec(memory_space=pltpu.HBM),
            pl.BlockSpec(memory_space=pltpu.SMEM),
            pl.BlockSpec(memory_space=pltpu.SMEM),
        ],
        out_specs=pl.BlockSpec(memory_space=pltpu.VMEM),
        scratch_shapes=[
            pltpu.VMEM((STEPS + 1, 2, planes + 2, half + EXT + 2 * PAD, nz), jnp.float32),
            pltpu.VMEM((planes, half + EXT, nz), jnp.float32),
            pltpu.VMEM((2, planes, half, nz), jnp.float32),
            pltpu.VMEM((planes, half, nz), jnp.float32),
            pltpu.VMEM((2, 2, 8, nz), jnp.float32),
            dma((planes + 1,)),
            dma,
            dma,
            dma((2,)),
            dma((2,)),
            dma((STEPS - 1, 2, 2)),
            dma((STEPS - 1, 2, 2)),
            dma((STEPS, 2)),
            dma((STEPS, 2)),
            dma((planes,)),
            dma((planes,)),
            dma((2, planes, 2)),
            dma((2, planes, 2)),
            dma((planes, 2)),
            dma((planes, 2)),
        ],
        compiler_params=pltpu.CompilerParams(
            collective_id=0, has_side_effects=True, vmem_limit_bytes=50 * 1024 * 1024
        ),
    )(field, mobility, fractions, sides)


def solution(mesh):
    return jax.shard_map(
        functools.partial(local, mesh.shape["image"], mesh.shape["space"]),
        mesh=mesh,
        in_specs=(P("image", "space", None, None), P("space", None, None), P("image"), P("image")),
        out_specs=P("image", "space", None, None),
        check_vma=False,
    )
```

time: 182 us -> 102 us (0.56)
  the two profiles are of different devices: /device:TPU:237 before, /device:TPU:217 now
where the time goes in v4:
time: 102 us
  Pallas kernels  99 us (97%)
  local copies, waits for them, and re-layouts  1.32 us (1%)
  between operations  1.3 us (1%)
    pallas_call x1, Pallas kernels, local(): pl.pallas_call(functools.partial(kernel, (images, spaces, planes, ny, nz)...  99 us

profile of v4, /device:TPU:217, one launch (start us, length us, event | category | flops | bytes accessed | tf_op | source)
XLA Modules:
  0.0 101.6 jit_solution(9391663166729414768)
XLA Ops:
  1.3 99.0 %shard_map.46 = f32[1,4,256,512]{3,2,1,0:T(8,128)S(1)} custom-call(f32[1,4,256,512]{3,2,1,0:T(8,128)} %field.1, f32[4,256,512]{2,1,0:T(8,128)} %mobility.1, f32[1]{0:T(128)S(6)} %copy.6.frac, s32[1]{0:T(128)S(6)} %copy.7.sides), custom_call_target="tpu_custom_call" | custom-call | tf_op jit(solution)/shard_map/pallas_call | solution.py:389
  100.3 1.3 %copy.8 = f32[1,4,256,512]{3,2,1,0:T(8,128)} copy(f32[1,4,256,512]{3,2,1,0:T(8,128)S(1)} %shard_map.46) | data formatting | bytes 4194304

commit v5 on v2

--- a/solution.py
+++ b/solution.py
@@ -314,7 +314,7 @@
 
     def step(t, _):
         def within(k, _):
-            a = lax.rem(hi + k, 2)
+            a = k
             for c in range(len(chunks)):
                 for p in inner:
                     advance(t, a, p, c)
@@ -323,7 +323,7 @@
         lax.fori_loop(0, 2, within, 0)
 
         def rim(k, _):
-            a = lax.rem(hi + k, 2)
+            a = k
             for c in range(len(chunks)):
                 wait_halo(t, a, c)
                 advance(t, a, first, c)
@@ -342,7 +342,7 @@
         return jnp.logical_and(img - 2 + 4 * a >= 0, img - 2 + 4 * a < images)
 
     def final_within(k, _):
-        a = lax.rem(hi + k, 2)
+        a = k
         for c in range(len(chunks)):
             for p in inner:
                 advance(end, a, p, c)
@@ -358,7 +358,7 @@
     lax.fori_loop(0, 2, final_within, 0)
 
     def final_rim(k, _):
-        a = lax.rem(hi + k, 2)
+        a = k
         for c in range(len(chunks)):
             wait_halo(end, a, c)
             advance(end, a, first, c)

time: 93 us -> 91.4 us (0.983)
  Pallas kernels: 90.2 us -> 88.6 us
    pallas_call x1, Pallas kernels: 90.2 us -> 88.6 us  [local(): pl.pallas_call(functools.partial(kernel, (images, spaces, planes, ny, nz)...]
where the time goes in v5:
time: 91.4 us; the launch traced here: 91.2 us
  Pallas kernels  88.6 us (97%)
  local copies, waits for them, and re-layouts  1.32 us (1%)
  between operations  1.3 us (1%)
    pallas_call x1, Pallas kernels, local(): pl.pallas_call(functools.partial(kernel, (images, spaces, planes, ny, nz)...  88.6 us

profile of v5, /device:TPU:219, one launch (start us, length us, event | category | flops | bytes accessed | tf_op | source)
XLA Modules:
  0.0 91.2 jit_solution(199039104655232882)
XLA Ops:
  1.3 88.6 %shard_map.46 = f32[1,4,256,512]{3,2,1,0:T(8,128)S(1)} custom-call(f32[1,4,256,512]{3,2,1,0:T(8,128)} %field.1, f32[4,256,512]{2,1,0:T(8,128)} %mobility.1, f32[1]{0:T(128)S(6)} %copy.6.frac, s32[1]{0:T(128)S(6)} %copy.7.sides), custom_call_target="tpu_custom_call" | custom-call | tf_op jit(solution)/shard_map/pallas_call | solution.py:444
  89.9 1.3 %copy.8 = f32[1,4,256,512]{3,2,1,0:T(8,128)} copy(f32[1,4,256,512]{3,2,1,0:T(8,128)S(1)} %shard_map.46) | data formatting | bytes 4194304

commit v6 on v5

--- a/solution.py
+++ b/solution.py
@@ -142,15 +142,6 @@
             flag = jnp.logical_and(flag, item)
         return pl.when(flag)
 
-    def send_halo(t, a, c):
-        @when(has_r)
-        def _():
-            halo(t, 0, a, c).start()
-
-        @when(has_l)
-        def _():
-            halo(t, 1, a, c).start()
-
     def wait_halo(t, a, c):
         @when(has_l)
         def _():
@@ -159,6 +150,27 @@
         @when(has_r)
         def _():
             halo(t, 1, a, c).wait_recv()
+
+    outer = jnp.where(core == 0, first, last)
+    near = first + last - outer
+
+    def send_face(t, a, c, out_side):
+        @when(core == (1 if out_side else 0), has_r)
+        def _():
+            halo(t, 0, a, c).start()
+
+        @when(core == (0 if out_side else 1), has_l)
+        def _():
+            halo(t, 1, a, c).start()
+
+    def wait_face(copy, out_side):
+        @when(core == (0 if out_side else 1), has_l)
+        def _():
+            copy(0).wait_recv()
+
+        @when(core == (1 if out_side else 0), has_r)
+        def _():
+            copy(1).wait_recv()
 
     def advance(t, a, p, c):
         r, n = chunks[c]
@@ -292,22 +304,17 @@
                     fcopy(i, p, other).wait_recv()
             send_in(other)
 
+        wait_face(lambda side: halo_in(side, a), True)
+        for c in range(len(chunks)):
+            advance(0, a, outer, c)
+            send_face(1, a, c, True)
         for c in range(len(chunks)):
             for p in inner:
                 advance(0, a, p, c)
-
-        @when(has_l)
-        def _():
-            halo_in(0, a).wait_recv()
-
-        @when(has_r)
-        def _():
-            halo_in(1, a).wait_recv()
-
+        wait_face(lambda side: halo_in(side, a), False)
         for c in range(len(chunks)):
-            advance(0, a, first, c)
-            advance(0, a, last, c)
-            send_halo(1, a, c)
+            advance(0, a, near, c)
+            send_face(1, a, c, False)
         return 0
 
     lax.fori_loop(0, 2, begin, 0)
@@ -322,16 +329,16 @@
 
         lax.fori_loop(0, 2, within, 0)
 
-        def rim(k, _):
-            a = k
-            for c in range(len(chunks)):
-                wait_halo(t, a, c)
-                advance(t, a, first, c)
-                advance(t, a, last, c)
-                send_halo(t + 1, a, c)
-            return 0
-
-        lax.fori_loop(0, 2, rim, 0)
+        for plane, out_side in ((outer, True), (near, False)):
+
+            def rim(a, _):
+                for c in range(len(chunks)):
+                    wait_face(lambda side: halo(t, side, a, c), out_side)
+                    advance(t, a, plane, c)
+                    send_face(t + 1, a, c, out_side)
+                return 0
+
+            lax.fori_loop(0, 2, rim, 0)
         return 0
 
     lax.fori_loop(1, STEPS - 1, step, 0)

time: 91.4 us -> 91 us (level)
  the two profiles are of different devices: /device:TPU:219 before, /device:TPU:225 now
where the time goes in v6:
time: 91 us; the launch traced here: 90.8 us
  Pallas kernels  88.2 us (97%)
  local copies, waits for them, and re-layouts  1.32 us (1%)
  between operations  1.3 us (1%)
    pallas_call x1, Pallas kernels, local(): pl.pallas_call(functools.partial(kernel, (images, spaces, planes, ny, nz)...  88.2 us

profile of v6, /device:TPU:225, one launch (start us, length us, event | category | flops | bytes accessed | tf_op | source)
XLA Modules:
  0.0 90.8 jit_solution(15325168820226546964)
XLA Ops:
  1.3 88.2 %shard_map.46 = f32[1,4,256,512]{3,2,1,0:T(8,128)S(1)} custom-call(f32[1,4,256,512]{3,2,1,0:T(8,128)} %field.1, f32[4,256,512]{2,1,0:T(8,128)} %mobility.1, f32[1]{0:T(128)S(6)} %copy.6.frac, s32[1]{0:T(128)S(6)} %copy.7.sides), custom_call_target="tpu_custom_call" | custom-call | tf_op jit(solution)/shard_map/pallas_call | solution.py:451
  89.5 1.3 %copy.8 = f32[1,4,256,512]{3,2,1,0:T(8,128)} copy(f32[1,4,256,512]{3,2,1,0:T(8,128)S(1)} %shard_map.46) | data formatting | bytes 4194304
